TPU v7x, 32 devices: a whole 2x2x4 slice. The times are simulated.
32 devices in a mesh: pb: 2 (over x), col: 16 (over z, y, core).
Axes of the slice: x: 2, y: 2, z: 4, core: 2. Of those that a mesh axis runs over, the one named last changes fastest.
Arguments:
- queries: bfloat16 [4096, 1024], P(('pb', 'col')), may hold values from -64 to 64
- candidates: bfloat16 [16384, 1024], P(('col', 'pb')), may hold values from -5 to 5
- grades: int32 [4096, 16384], P('pb', 'col'), may hold values from 0 to 4
- query_weights: float32 [4096], P('pb'), may hold values from -0.046875 to 0.046875
Outputs:
- losses: float32 [4096], P('pb')
- query_grad: bfloat16 [4096, 1024], P(('pb', 'col'))
- cand_grad: bfloat16 [16384, 1024], P(('col', 'pb'))
All inputs are finite; a program needn't handle non-finite values.
Results may differ from a plain program's by a relative error of at most 0.0071.
Values may be sent and summed in bfloat16 or wider, within the bound.
A program may use at most 128 MiB of HBM per device.

v0:
```python
import math

import jax
import jax.numpy as jnp
from jax import lax
from jax.sharding import PartitionSpec as P

GRADES = 5


lowest = -1e30


def combined_all(x, axis, combine):
    everything = jax.tree.map(lambda part: lax.all_gather(part, axis), x)
    leading = jax.tree.map(lambda part: part[0], everything)

    def step(k, so_far):
        return combine(so_far, jax.tree.map(lambda part: part[k], everything))

    return lax.fori_loop(1, lax.axis_size(axis), step, leading)


def grade_levels(maxima, masses, counts):
    levels = []
    running = maxima[0]
    seen_count = counts[0] * 0.0
    for bucket in range(maxima.shape[0]):
        running = jnp.maximum(running, maxima[bucket])
        seen_count = seen_count + counts[bucket]
        summed = masses[0] * jnp.exp(maxima[0] - running)
        for lesser in range(1, bucket + 1):
            summed = summed + masses[lesser] * jnp.exp(maxima[lesser] - running)
        present = seen_count > 0.0
        levels.append(
            jnp.where(present, running + jnp.log(jnp.where(present, summed, 1.0)), running)
        )
    return levels


def slope_factors(maxima, levels, counts):
    factors = []
    for bucket in range(maxima.shape[0]):
        summed = counts[bucket] * jnp.exp(maxima[bucket] - levels[bucket])
        for higher in range(bucket + 1, maxima.shape[0]):
            summed = summed + counts[higher] * jnp.exp(maxima[bucket] - levels[higher])
        factors.append(summed)
    return factors


def local(queries, candidates, grades, query_weights):
    width = queries.shape[1]
    scaling = 1.0 / math.sqrt(width)
    cand_block = lax.all_gather(candidates, "pb", axis=0, tiled=True)
    query_block = lax.all_gather(queries, "col", axis=0, tiled=True)
    scores = jnp.dot(query_block, cand_block.T, preferred_element_type=jnp.float32) * scaling
    members = [grades == bucket for bucket in range(GRADES)]
    totals_local = jnp.sum(scores, axis=1)
    counts_local = jnp.stack([jnp.sum(member.astype(jnp.float32), axis=1) for member in members])
    maxima_local = jnp.stack(
        [jnp.max(jnp.where(member, scores, lowest), axis=1) for member in members]
    )

    def spread_rows(values):
        picked = jnp.zeros(scores.shape, jnp.float32)
        for bucket in range(GRADES):
            picked = jnp.where(members[bucket], values[bucket][:, None], picked)
        return picked

    def masses_from(expo):
        return jnp.stack(
            [jnp.sum(jnp.where(members[bucket], expo, 0.0), axis=1) for bucket in range(GRADES)]
        )

    def combine(former, latter):
        merged = jnp.maximum(former[0], latter[0])
        rescaled = former[1] * jnp.exp(former[0] - merged) + latter[1] * jnp.exp(latter[0] - merged)
        return (merged, rescaled, former[2] + latter[2], former[3] + latter[3])

    expo = jnp.exp(scores - spread_rows(maxima_local))
    maxima, masses, counts, totals = combined_all(
        (maxima_local, masses_from(expo), counts_local, totals_local), "col", combine
    )
    columns_all = grades.shape[1] * lax.axis_size("col")
    levels = grade_levels(maxima, masses, counts)
    weighted = counts[0] * levels[0]
    for bucket in range(1, GRADES):
        weighted = weighted + counts[bucket] * levels[bucket]
    losses = (weighted - totals) / columns_all
    factors = jnp.stack(slope_factors(maxima, levels, counts))
    scaled_factors = factors * jnp.exp(maxima_local - maxima)
    slopes = (query_weights[:, None] * (spread_rows(scaled_factors) * expo - 1.0)).astype(
        jnp.bfloat16
    )
    query_grad = lax.psum_scatter(
        jnp.dot(slopes, cand_block, preferred_element_type=jnp.float32) * scaling,
        "col",
        scatter_dimension=0,
        tiled=True,
    ).astype(jnp.bfloat16)
    cand_grad = lax.psum_scatter(
        lax.dot_general(
            slopes, query_block, (((0,), (0,)), ((), ())), preferred_element_type=jnp.float32
        )
        * scaling,
        "pb",
        scatter_dimension=0,
        tiled=True,
    )
    return (losses, query_grad, cand_grad.astype(jnp.bfloat16))


def solution(mesh):
    in_specs = (P(("pb", "col"), None), P(("col", "pb"), None), P("pb", "col"), P("pb"))
    out_specs = (P("pb"), P(("pb", "col"), None), P(("col", "pb"), None))
    return jax.shard_map(local, mesh=mesh, in_specs=in_specs, out_specs=out_specs, check_vma=False)
```

profile of v0, /device:TPU:0, one launch (start us, length us, event | category | flops | bytes accessed | tf_op | source)
XLA Modules:
  0.0 426.9 jit_solution(16694783811220427614)
XLA Ops:
  7.2 0.0 all-gather.12.cloned.1.call-start
  7.2 0.7 all-gather.12.cloned.1.call-update
  7.9 0.0 all-gather.10.cloned.1.call-start
  7.9 0.7 all-gather.10.cloned.1.call-update
  8.6 0.0 reduce-scatter.5.cloned.1.call-start
  8.7 9.1 %copy.14 = s32[2048,1024]{0,1:T(8,128)} copy(s32[2048,1024]{1,0:T(8,128)} %param.8) | data formatting | bytes 16777216 | tf_op args[2]
  17.8 27.5 %all-gather.12.cloned.1.call-done = bf16[1024,1024]{1,0:T(8,128)(2,1)} async-done(((bf16[512,1024]{1,0:T(8,128)(2,1)}), bf16[1024,1024]{1,0:T(8,128)(2,1)}) %all-gather.12.cloned.1.call-update) | async-done | bytes 2097168 | tf_op jit(solution)/shard_map/all_gather | solution.py:54
  45.4 52.6 %all-gather.10.cloned.1.call-done = bf16[2048,1024]{1,0:T(8,128)(2,1)} async-done(((bf16[128,1024]{1,0:T(8,128)(2,1)}), bf16[2048,1024]{1,0:T(8,128)(2,1)}) %all-gather.10.cloned.1.call-update) | async-done | bytes 4194320 | tf_op jit(solution)/shard_map/all_gather | solution.py:55
  97.9 19.5 %multiply_reduce_fusion = (f32[2048]{0:T(1024)S(1)}, f32[2048]{0:T(1024)S(1)}, f32[2048]{0:T(1024)S(1)}, f32[2048]{0:T(1024)S(1)}, f32[2048]{0:T(1024)S(1)}, /*i...) fusion(s32[2048,1024]{0,1:T(8,128)} %copy.14, ...), kind=kOutput, calls=%fused_computation.24 | convolution fusion | flops 4334798848 | bytes 33611776 | tf_op jit(solution)/shard_map/dot_general | solution.py:56
  117.5 0.0 copy-start.5
  117.5 0.0 copy-start.6
  117.5 19.3 %all-gather.3 = f32[32768]{0:T(1024)S(1)} all-gather(f32[2048]{0:T(1024)S(1)} %get-tuple-element.236), channel_id=5, replica_groups=mesh['pb'=2,'col'=16] {'col'}, dimensions={0}, use_global_device_ids=true | all-gather | bytes 139264 | tf_op jit(solution)/shard_map/all_gather | solution.py:15
  136.8 16.7 %select_reduce_fusion = (f32[2048]{0:T(1024)S(1)}, f32[2048]{0:T(1024)S(1)}, f32[2048]{0:T(1024)S(1)}, f32[2048]{0:T(1024)S(1)}, f32[2048]{0:T(1024)}, /*index=5...) fusion(pred[2048,1024]{0,1:T(8,128)(4,1)} %get-tuple-element.282, ...), kind=kLoop, calls=%fused_computation.13 | loop fusion | flops 52410368 | bytes 27377664 | tf_op jit(solution)/shard_map/reduce_sum | solution.py:72
  153.5 0.0 copy-done.3
  153.5 0.0 copy-done.4
  153.5 0.0 copy-done.5
  153.5 0.0 copy-done.6
  153.5 0.1 stack.79
  153.6 20.8 %all-gather.6 = f32[16,5,2048]{2,1,0:T(8,128)S(1)} all-gather(f32[1,5,2048]{2,1,0:T(8,128)S(1)} %bitcast.71), channel_id=4, replica_groups=mesh['pb'=2,'col'=16] {'col'}, dimensions={0}, use_global_device_ids=true | all-gather | bytes 696320 | tf_op jit(solution)/shard_map/all_gather | solution.py:15
  174.4 0.8 stack.73
  175.2 25.6 %all-gather.5 = f32[16,5,2048]{2,1,0:T(8,128)S(1)} all-gather(f32[1,5,2048]{2,1,0:T(8,128)S(1)} %bitcast.72), channel_id=3, replica_groups=mesh['pb'=2,'col'=16] {'col'}, dimensions={0}, use_global_device_ids=true | all-gather | bytes 696320 | tf_op jit(solution)/shard_map/all_gather | solution.py:15
  200.8 1.1 copy-done.1
  201.8 0.8 stack.67
  202.6 20.7 %all-gather.4 = f32[16,5,2048]{2,1,0:T(8,128)S(1)} all-gather(f32[1,5,2048]{2,1,0:T(8,128)S(1)} %bitcast.70), channel_id=2, replica_groups=mesh['pb'=2,'col'=16] {'col'}, dimensions={0}, use_global_device_ids=true | all-gather | bytes 696320 | tf_op jit(solution)/shard_map/all_gather | solution.py:15
  223.3 1.0 copy-done.2
  224.3 15.0 %while.21 = (s32[]{:T(128)}, f32[5,2048]{1,0:T(8,128)S(1)}, f32[5,2048]{1,0:T(8,128)S(1)}, f32[5,2048]{1,0:T(8,128)S(1)}, f32[2048]{0:T(1024)S(1)}, /*index=5*/f...) while((s32[]{:T(128)}, f32[5,2048]{1,0:T(8,128)S(1)}, ...), condition=%wide.region_17.18_spmd, body=%wide.region_16.17_spmd.sunk | while | flops 73733 | bytes 409767 | solution.py:21
  224.3 0.9 fusion.46
  225.3 0.9 fusion.46
  226.3 0.9 fusion.46
  227.3 0.9 fusion.46
  228.3 0.9 fusion.46
  229.3 0.9 fusion.46
  230.3 0.9 fusion.46
  231.3 0.9 fusion.46
  232.3 0.9 fusion.46
  233.3 0.9 fusion.46
  234.3 0.9 fusion.46
  235.3 0.9 fusion.46
  236.3 0.9 fusion.46
  237.3 0.9 fusion.46
  238.3 0.9 fusion.46
  239.3 0.2 exponential_multiply_fusion.1
  239.5 0.2 multiply_add_fusion.2
  239.7 0.1 multiply_add_fusion.3
  239.8 0.1 multiply_add_fusion.4
  239.9 0.2 multiply_add_fusion.5
  240.1 0.1 stack.80
  240.2 0.0 copy-start.7
  240.2 8.7 %multiply_convert_fusion = bf16[2048,1024]{0,1:T(8,128)(2,1)S(1)} fusion(f32[2048,1024]{0,1:T(8,128)} %get-tuple-element.280, pred[2048,1024]{0,1:T(8,128)(4,1)} %get-tuple-element.282, pred[2048,1024]{0,1:T(8,128)(4,1)} %get-tuple-element.283, pred[2048,1024]{0,1:T(8,128)(4,1)} %get-tuple-element.284, pred[2048,1024]{0,1:T(8,128)(4,1)} %get-tuple-element.285, ...), kind=kLoop, calls=%fused_computation.7 | loop fusion | flops 18874368 | bytes 23117824 | tf_op jit(solution)/shard_map/convert_element_type | solution.py:92
  249.0 0.0 copy-start
  249.0 2.0 copy-done
  250.9 0.0 copy-done.7
  250.9 6.0 %convolution_multiply_fusion.1 = f32[1024,1024]{1,0:T(8,128)} fusion(bf16[2048,1024]{0,1:T(8,128)(2,1)S(1)} %multiply_convert_fusion, bf16[2048,1024]{1,0:T(8,128)(2,1)S(1)} %copy-done.7), kind=kOutput, calls=%fused_computation.31 | convolution fusion | flops 4296015872 | bytes 12582912 | tf_op jit(solution)/shard_map/dot_general | solution.py:102
  257.0 0.0 reduce-scatter.5.cloned.1.call-update
  257.0 0.0 reduce-scatter.3.cloned.1.call-start
  257.0 0.0 copy-done.8
  257.0 9.0 %convolution_multiply_fusion = f32[2048,1024]{0,1:T(8,128)} fusion(bf16[2048,1024]{0,1:T(8,128)(2,1)} %copy-done, bf16[1024,1024]{1,0:T(8,128)(2,1)S(1)} %copy-done.8), kind=kOutput, calls=%fused_computation.25 | convolution fusion | flops 4297064448 | bytes 14680064 | tf_op jit(solution)/shard_map/dot_general | solution.py:96
  266.0 0.0 reduce-scatter.3.cloned.1.call-update
  266.1 0.7 fusion.9
  266.7 44.2 %reduce-scatter.5.cloned.1.call-done = f32[512,1024]{1,0:T(8,128)} async-done(((f32[1024,1024]{1,0:T(8,128)}), f32[512,1024]{1,0:T(8,128)}) %reduce-scatter.5.cloned.1.call-update) | async-done | bytes 2097168 | tf_op jit(solution)/shard_map/reduce_scatter | solution.py:101
  310.9 2.7 convert_element_type.31
  313.7 104.8 %reduce-scatter.3.cloned.1.call-done = f32[128,1024]{0,1:T(8,128)} async-done(((f32[2048,1024]{0,1:T(8,128)}), f32[128,1024]{0,1:T(8,128)}) %reduce-scatter.3.cloned.1.call-update) | async-done | bytes 524304 | tf_op jit(solution)/shard_map/reduce_scatter | solution.py:95
  418.5 1.1 convert_element_type.30
  419.5 0.8 copy.20
  (42 shorter events, 0.4 us)
Async XLA Ops:
  7.2 38.2 %all-gather.12.cloned.1.call-start = ((), (), s32[]{:S(2)}) async-start(), calls=%async_computation.3 | async-start | bytes 3145728 | tf_op jit(solution)/shard_map/all_gather | solution.py:54
  7.9 90.0 %all-gather.10.cloned.1.call-start = ((), (), s32[]{:S(2)}) async-start(), calls=%async_computation.2 | async-start | bytes 4456448 | tf_op jit(solution)/shard_map/all_gather | solution.py:55
  8.6 302.3 %reduce-scatter.5.cloned.1.call-start = ((), (), s32[]{:S(2)}) async-start(), calls=%async_computation.5 | async-start | bytes 6291456 | tf_op jit(solution)/shard_map/reduce_scatter | solution.py:101
  117.5 36.0 %copy-start.3 = (f32[2048]{0:T(1024)}, f32[2048]{0:T(1024)S(1)}, u32[]{:S(2)}) copy-start(f32[2048]{0:T(1024)S(1)} %get-tuple-element.238) | copy-start | bytes 24580
  117.5 36.0 %copy-start.4 = (f32[2048]{0:T(1024)}, f32[2048]{0:T(1024)S(1)}, u32[]{:S(2)}) copy-start(f32[2048]{0:T(1024)S(1)} %get-tuple-element.239) | copy-start | bytes 24580
  117.5 36.0 %copy-start.5 = (f32[2048]{0:T(1024)}, f32[2048]{0:T(1024)S(1)}, u32[]{:S(2)}) copy-start(f32[2048]{0:T(1024)S(1)} %get-tuple-element.240) | copy-start | bytes 24580
  117.5 36.0 %copy-start.6 = (f32[2048]{0:T(1024)}, f32[2048]{0:T(1024)S(1)}, u32[]{:S(2)}) copy-start(f32[2048]{0:T(1024)S(1)} %get-tuple-element.241) | copy-start | bytes 24580
  200.8 1.1 copy-start.1
  223.3 1.0 copy-start.2
  240.2 10.7 %copy-start.7 = (bf16[2048,1024]{1,0:T(8,128)(2,1)S(1)}, bf16[2048,1024]{1,0:T(8,128)(2,1)}, u32[]{:S(2)}) copy-start(bf16[2048,1024]{1,0:T(8,128)(2,1)} %all-gather.10.cloned.1.call-done) | copy-start | bytes 12582916
  249.0 2.0 copy-start
  250.9 6.1 %copy-start.8 = (bf16[1024,1024]{1,0:T(8,128)(2,1)S(1)}, bf16[1024,1024]{1,0:T(8,128)(2,1)}, u32[]{:S(2)}) copy-start(bf16[1024,1024]{1,0:T(8,128)(2,1)} %all-gather.12.cloned.1.call-done) | copy-start | bytes 6291460
  257.0 161.5 %reduce-scatter.3.cloned.1.call-start = ((), (), s32[]{:S(2)}) async-start(), calls=%async_computation.4 | async-start | bytes 8912896 | tf_op jit(solution)/shard_map/reduce_scatter | solution.py:95
Sparse Core Ops, SparseCore 0:
  9.5 35.8 all-gather.11
  47.5 50.3 all-gather.9
  257.1 53.7 reduce-scatter.4
  314.9 103.5 reduce-scatter.2
where the time goes:
time: 428 us; the launch traced here: 427 us
  waiting for transfers between devices  231 us (54%)
  blocking collectives  86.4 us (20%)
  other arithmetic  44.8 us (10%)
  matrix products  34.6 us (8%)
  local copies, waits for them, and re-layouts  16 us (4%)
  between operations  13.9 us (3%)
    reduce_scatter x1, waiting for transfers between devices, local(): lax.psum_scatter(jnp.dot(slopes, cand_block, preferred_element_type=jnp.f...  105 us
    all_gather x4, blocking collectives, combined_all(): everything = jax.tree.map(lambda part: lax.all_gather(part, axis), x)  86.4 us
    all_gather x1, waiting for transfers between devices, local(): query_block = lax.all_gather(queries, 'col', axis=0, tiled=True)  52.6 us
    reduce_scatter x1, waiting for transfers between devices, local(): lax.psum_scatter(lax.dot_general(slopes, query_block, (((0,), (0,)), ((),...  44.2 us
    all_gather x1, waiting for transfers between devices, local(): cand_block = lax.all_gather(candidates, 'pb', axis=0, tiled=True)  27.5 us
    dot_general x1, matrix products, local(): jnp.dot(query_block, cand_block.T, preferred_element_type=jnp.float32)  19.5 us
    reduce_sum x1, other arithmetic, masses_from(): jnp.sum(jnp.where(members[bucket], expo, 0.0), axis=1)  16.7 us
    add x15, other arithmetic, combine(): former[1] * jnp.exp(former[0] - merged)  14.2 us
  transfers between devices with their start and end apart: 4, of which 4 were waited for; matrix products, arithmetic and copies ran while one was open for 5% of the time, Pallas kernels for 0%

commit v1 on v0

v1 whole, which is shorter than its diff:
```python
import functools
import math

import jax
import jax.numpy as jnp
from jax import lax
from jax.experimental import pallas as pl
from jax.experimental.pallas import tpu as pltpu
from jax.sharding import PartitionSpec as P

GRADES = 5
STATS = 16
LOWEST = -1e30
MESH = pl.DeviceIdType.MESH
F32 = jnp.float32
BF16 = jnp.bfloat16


def dev(p, i):
    return {"pb": p, "col": i}


class Place:
    def __init__(self, n_col, n_pb):
        self.n_col, self.n_pb = n_col, n_pb
        self.cores = 2 if n_col % 2 == 0 else 1
        rest = n_col // self.cores
        self.mids = 2 if rest % 2 == 0 else 1
        self.outs = rest // self.mids
        self.me = lax.axis_index("col")
        self.p = lax.axis_index("pb")
        self.core = lax.rem(self.me, self.cores)
        chip = self.me // self.cores
        self.mid = lax.rem(chip, self.mids)
        self.out = chip // self.mids

    def index(self, do, dm, dc):
        o = lax.rem(self.out + do, self.outs)
        m = lax.rem(self.mid + dm, self.mids)
        c = lax.rem(self.core + dc, self.cores)
        return (o * self.mids + m) * self.cores + c

    def peers(self):
        found = [dev(self.p, self.index(d, 0, 0)) for d in range(1, self.outs)]
        found += [dev(self.p, self.index(0, d, 0)) for d in range(1, self.mids)]
        found += [dev(self.p, self.index(0, 0, d)) for d in range(1, self.cores)]
        found += [dev(lax.rem(self.p + d, self.n_pb), self.me) for d in range(1, self.n_pb)]
        return found


def greet(peers):
    barrier = pltpu.get_barrier_semaphore()
    for peer in peers:
        pl.semaphore_signal(barrier, inc=1, device_id=peer, device_id_type=MESH)
    pl.semaphore_wait(barrier, len(peers))


def remote(src, dst, send, recv, device):
    return pltpu.make_async_remote_copy(
        src_ref=src, dst_ref=dst, send_sem=send, recv_sem=recv, device_id=device, device_id_type=MESH
    )


def gather_kernel(n_col, n_pb, q_ref, c_ref, q_all, c_all, q_send, q_recv, c_send, c_recv, own_sem):
    at = Place(n_col, n_pb)
    own = [
        pltpu.make_async_copy(q_ref, q_all.at[at.me], own_sem.at[0]),
        pltpu.make_async_copy(c_ref, c_all.at[at.p], own_sem.at[1]),
    ]
    for copy in own:
        copy.start()
    greet(at.peers())
    c_copies = []
    for d in range(1, n_pb):
        other = lax.rem(at.p + d, n_pb)
        copy = remote(c_ref, c_all.at[at.p], c_send.at[d], c_recv.at[at.p], dev(other, at.me))
        copy.start()
        c_copies.append(copy)
    sends = []

    def push(src, block, device):
        copy = remote(src, q_all.at[block], q_send.at[len(sends)], q_recv.at[block], device)
        copy.start()
        sends.append(copy)

    def arrived(block):
        remote(q_ref, q_all.at[block], q_send.at[0], q_recv.at[block], dev(at.p, at.me)).wait_recv()

    def spread(do, dm):
        block = at.index(do, dm, 0)
        if do or dm:
            arrived(block)
            src = q_all.at[block]
        else:
            src = q_ref
        if dm == 0:
            if do == 0:
                for d in range(1, at.outs):
                    push(src, block, dev(at.p, at.index(d, 0, 0)))
            for d in range(1, at.mids):
                push(src, block, dev(at.p, at.index(0, d, 0)))
        for d in range(1, at.cores):
            push(src, block, dev(at.p, at.index(0, 0, d)))

    order = [0] + sorted(range(1, at.outs), key=lambda d: min(d, at.outs - d))
    for do in order:
        spread(do, 0)
    for do in order:
        for dm in range(1, at.mids):
            spread(do, dm)
    for d in range(1, at.cores):
        for do in order:
            for dm in range(at.mids):
                arrived(at.index(do, dm, d))
    for d in range(1, n_pb):
        other = lax.rem(at.p + d, n_pb)
        remote(c_ref, c_all.at[other], c_send.at[0], c_recv.at[other], dev(at.p, at.me)).wait_recv()
    for copy in sends + c_copies:
        copy.wait_send()
    for copy in own:
        copy.wait()


def gather(q, c, n_col, n_pb):
    vmem = pl.BlockSpec(memory_space=pltpu.VMEM)
    hbm = pl.BlockSpec(memory_space=pl.ANY)
    return pl.pallas_call(
        functools.partial(gather_kernel, n_col, n_pb),
        out_shape=(
            jax.ShapeDtypeStruct((n_col, *q.shape), q.dtype),
            jax.ShapeDtypeStruct((n_pb, *c.shape), c.dtype),
        ),
        in_specs=[vmem, vmem],
        out_specs=(hbm, hbm),
        scratch_shapes=[
            pltpu.SemaphoreType.DMA((2 * n_col,)),
            pltpu.SemaphoreType.DMA((n_col,)),
            pltpu.SemaphoreType.DMA((n_pb,)),
            pltpu.SemaphoreType.DMA((n_pb,)),
            pltpu.SemaphoreType.DMA((2,)),
        ],
        compiler_params=pltpu.CompilerParams(collective_id=0, has_side_effects=True),
        name="gather",
    )(q, c)


def score_kernel(scaling, q_ref, c_ref, g_ref, e_ref, s_ref):
    rows = g_ref.shape[0]
    scores = (
        lax.dot_general(
            q_ref[0], c_ref[...], (((1,), (1,)), ((), ())), preferred_element_type=F32
        )
        * scaling
    )
    grades = g_ref[...]
    lane = lax.broadcasted_iota(jnp.int32, (rows, rows), 1)
    table = jnp.zeros((rows, rows), F32)
    picked = jnp.zeros(scores.shape, F32)
    for b in range(GRADES):
        member = grades == b
        highest = jnp.max(jnp.where(member, scores, LOWEST), axis=1, keepdims=True)
        picked = jnp.where(member, highest, picked)
        table = jnp.where(lane == b, highest, table)
    expo = jnp.exp(scores - picked)
    e_ref[...] = expo
    for b in range(GRADES):
        member = grades == b
        mass = jnp.sum(jnp.where(member, expo, 0.0), axis=1, keepdims=True)
        count = jnp.sum(jnp.where(member, 1.0, 0.0), axis=1, keepdims=True)
        table = jnp.where(lane == GRADES + b, mass, table)
        table = jnp.where(lane == 2 * GRADES + b, count, table)
    total = jnp.sum(scores, axis=1, keepdims=True)
    table = jnp.where(lane == 3 * GRADES, total, table)
    s_ref[0] = table.T[:STATS]


def score(q_all, c_block, grades, scaling):
    n, rows, width = q_all.shape
    cols = c_block.shape[0]
    return pl.pallas_call(
        functools.partial(score_kernel, scaling),
        grid=(n,),
        out_shape=(
            jax.ShapeDtypeStruct(grades.shape, F32),
            jax.ShapeDtypeStruct((n, STATS, rows), F32),
        ),
        in_specs=[
            pl.BlockSpec((1, rows, width), lambda i: (i, 0, 0)),
            pl.BlockSpec((cols, width), lambda i: (0, 0)),
            pl.BlockSpec((rows, cols), lambda i: (i, 0)),
        ],
        out_specs=(
            pl.BlockSpec((rows, cols), lambda i: (i, 0)),
            pl.BlockSpec((1, STATS, rows), lambda i: (i, 0, 0)),
        ),
        compiler_params=pltpu.CompilerParams(vmem_limit_bytes=40 * 2**20),
        name="score",
    )(q_all, c_block, grades)


def merge_kernel(n_col, columns, s_ref, all_ref, got, mine, send, recv, send2, recv2):
    me = lax.axis_index("col")
    p = lax.axis_index("pb")
    others = [lax.rem(me + d, n_col) for d in range(1, n_col)]
    greet([dev(p, o) for o in others])
    copies = []
    for d, o in enumerate(others):
        copy = remote(s_ref.at[o], got.at[me], send.at[d], recv.at[me], dev(p, o))
        copy.start()
        copies.append(copy)
    got[me] = s_ref[me]
    for o in others:
        remote(s_ref.at[o], got.at[o], send.at[0], recv.at[o], dev(p, o)).wait_recv()
    G = GRADES
    maxima = got[0][:G]
    for k in range(1, n_col):
        maxima = jnp.maximum(maxima, got[k][:G])
    masses = jnp.zeros_like(maxima)
    rest = jnp.zeros((STATS - 2 * G, maxima.shape[1]), F32)
    for k in range(n_col):
        block = got[k]
        masses = masses + block[G : 2 * G] * jnp.exp(block[:G] - maxima)
        rest = rest + block[2 * G :]
    mx = [maxima[b : b + 1] for b in range(G)]
    ms = [masses[b : b + 1] for b in range(G)]
    ct = [rest[b : b + 1] for b in range(G)]
    total = rest[G : G + 1]
    levels = []
    running = mx[0]
    seen = ct[0] * 0.0
    for b in range(G):
        running = jnp.maximum(running, mx[b])
        seen = seen + ct[b]
        summed = ms[0] * jnp.exp(mx[0] - running)
        for h in range(1, b + 1):
            summed = summed + ms[h] * jnp.exp(mx[h] - running)
        present = seen > 0.0
        levels.append(jnp.where(present, running + jnp.log(jnp.where(present, summed, 1.0)), running))
    weighted = ct[0] * levels[0]
    for b in range(1, G):
        weighted = weighted + ct[b] * levels[b]
    loss = (weighted - total) / columns
    factors = []
    for h in range(G):
        f = ct[h] * jnp.exp(mx[h] - levels[h])
        for b in range(h + 1, G):
            f = f + ct[b] * jnp.exp(mx[h] - levels[b])
        factors.append(f)
    pad = jnp.zeros((STATS - 2 * G - 1, loss.shape[1]), F32)
    mine[...] = jnp.concatenate(mx + factors + [loss, pad], axis=0)
    more = []
    for d, o in enumerate(others):
        copy = remote(mine, all_ref.at[me], send2.at[d], recv2.at[me], dev(p, o))
        copy.start()
        more.append(copy)
    all_ref[me] = mine[...]
    for o in others:
        remote(mine, all_ref.at[o], send2.at[0], recv2.at[o], dev(p, o)).wait_recv()
    for copy in copies + more:
        copy.wait_send()


def merge(stats, columns):
    n_col, _, rows = stats.shape
    vmem = pl.BlockSpec(memory_space=pltpu.VMEM)
    return pl.pallas_call(
        functools.partial(merge_kernel, n_col, columns),
        out_shape=jax.ShapeDtypeStruct(stats.shape, F32),
        in_specs=[vmem],
        out_specs=vmem,
        scratch_shapes=[
            pltpu.VMEM(stats.shape, F32),
            pltpu.VMEM((STATS, rows), F32),
            pltpu.SemaphoreType.DMA((n_col,)),
            pltpu.SemaphoreType.DMA((n_col,)),
            pltpu.SemaphoreType.DMA((n_col,)),
            pltpu.SemaphoreType.DMA((n_col,)),
        ],
        compiler_params=pltpu.CompilerParams(collective_id=1, has_side_effects=True),
        name="merge",
    )(stats)


def slope_kernel(scaling, per, e_ref, g_ref, q_ref, c_ref, s_ref, f_ref, w_ref, qg_ref, cg_ref, acc):
    step = pl.program_id(0)
    G = GRADES
    rows = s_ref.shape[2]
    pieces = []
    for k in range(per):
        local, merged, weight = s_ref[k], f_ref[k], w_ref[k]
        scaled = weight * (merged[G : 2 * G] * jnp.exp(local[:G] - merged[:G]))
        table = jnp.concatenate([scaled, weight, jnp.zeros((rows - G - 1, rows), F32)], axis=0).T
        grades = g_ref[k * rows : (k + 1) * rows]
        picked = jnp.broadcast_to(table[:, 0:1], grades.shape)
        for b in range(1, G):
            picked = jnp.where(grades == b, table[:, b : b + 1], picked)
        slopes = picked * e_ref[k * rows : (k + 1) * rows] - table[:, G : G + 1]
        pieces.append(slopes.astype(BF16))
    slopes = jnp.concatenate(pieces, axis=0)
    part = jnp.dot(slopes, c_ref[...], preferred_element_type=F32) * scaling
    qg_ref[...] = part.astype(BF16).reshape(qg_ref.shape)
    term = lax.dot_general(
        slopes,
        q_ref[...].reshape(per * rows, -1),
        (((0,), (0,)), ((), ())),
        preferred_element_type=F32,
    )

    @pl.when(step == 0)
    def _():
        acc[...] = term

    @pl.when(step > 0)
    def _():
        acc[...] += term

    @pl.when(step == pl.num_programs(0) - 1)
    def _():
        cg_ref[...] = (acc[...] * scaling).astype(BF16)


def slope(expo, grades, q_all, c_block, stats, merged, weights, scaling):
    n, rows, width = q_all.shape
    cols = c_block.shape[0]
    per = 2 if n % 2 == 0 else 1
    block3 = lambda a, b: pl.BlockSpec((per, a, b), lambda i: (i, 0, 0))
    return pl.pallas_call(
        functools.partial(slope_kernel, scaling, per),
        grid=(n // per,),
        out_shape=(
            jax.ShapeDtypeStruct((n, rows, width), BF16),
            jax.ShapeDtypeStruct((cols, width), BF16),
        ),
        in_specs=[
            pl.BlockSpec((per * rows, cols), lambda i: (i, 0)),
            pl.BlockSpec((per * rows, cols), lambda i: (i, 0)),
            block3(rows, width),
            pl.BlockSpec((cols, width), lambda i: (0, 0)),
            block3(STATS, rows),
            block3(STATS, rows),
            block3(1, rows),
        ],
        out_specs=(block3(rows, width), pl.BlockSpec((cols, width), lambda i: (0, 0))),
        scratch_shapes=[pltpu.VMEM((cols, width), F32)],
        compiler_params=pltpu.CompilerParams(vmem_limit_bytes=48 * 2**20),
        name="slope",
    )(expo, grades, q_all, c_block, stats, merged, weights)


def scatter_kernel(
    n_col, n_pb, qg, cg, q_out, c_out,
    core_got, acc, mid_got, out_got, c_got,
    core_send, core_recv, mid_send, mid_recv, out_send, out_recv, c_send, c_recv,
):
    at = Place(n_col, n_pb)
    greet(at.peers())
    copies = []

    def push(*args):
        copy = remote(*args)
        copy.start()
        copies.append(copy)

    for d in range(1, n_pb):
        other = lax.rem(at.p + d, n_pb)
        push(cg.at[other], c_got.at[d - 1], c_send.at[d], c_recv.at[d - 1], dev(other, at.me))
    order = sorted(range(1, at.outs), key=lambda d: min(d, at.outs - d)) + [0]
    far = [(do, dm) for do in order for dm in range(1, at.mids)] + [(do, 0) for do in order]
    slot = {pair: k for k, pair in enumerate(far)}
    for do, dm in far:
        k = slot[do, dm]
        if at.cores > 1:
            push(
                qg.at[at.index(do, dm, 1)], core_got.at[k], core_send.at[k], core_recv.at[k],
                dev(at.p, at.index(0, 0, 1)),
            )

    def core_sum(do, dm):
        k = slot[do, dm]
        own = qg[at.index(do, dm, 0)].astype(F32)
        if at.cores > 1:
            remote(core_got.at[k], core_got.at[k], core_send.at[k], core_recv.at[k], dev(at.p, at.me)).wait_recv()
            own = own + core_got[k].astype(F32)
        return own

    for do in order:
        for dm in range(1, at.mids):
            k = slot[do, dm]
            acc[k] = core_sum(do, dm).astype(BF16)
            push(acc.at[k], mid_got.at[k], mid_send.at[k], mid_recv.at[k], dev(at.p, at.index(0, dm, 0)))
    for do in order:
        k = slot[do, 0]
        acc[k] = core_sum(do, 0).astype(BF16)
    for do in order:
        k = slot[do, 0]
        total = acc[k].astype(F32)
        for dm in range(1, at.mids):
            j = slot[do, dm]
            remote(acc.at[j], mid_got.at[j], mid_send.at[j], mid_recv.at[j], dev(at.p, at.me)).wait_recv()
            total = total + mid_got[j].astype(F32)
        if do:
            acc[k] = total.astype(BF16)
            push(acc.at[k], out_got.at[do - 1], out_send.at[do - 1], out_recv.at[do - 1], dev(at.p, at.index(do, 0, 0)))
    for d in range(1, at.outs):
        remote(acc.at[0], out_got.at[d - 1], out_send.at[d - 1], out_recv.at[d - 1], dev(at.p, at.me)).wait_recv()
        total = total + out_got[d - 1].astype(F32)
    q_out[...] = total.astype(BF16)
    for d in range(1, n_pb):
        remote(cg.at[0], c_got.at[d - 1], c_send.at[d], c_recv.at[d - 1], dev(at.p, at.me)).wait_recv()
    half = 128
    for r in range(0, c_out.shape[0], half):
        rows = pl.ds(r, half)
        c_total = cg[at.p, rows].astype(F32)
        for d in range(1, n_pb):
            c_total = c_total + c_got[d - 1, rows].astype(F32)
        c_out[rows] = c_total.astype(BF16)
    for copy in copies:
        copy.wait_send()


def scatter(qg, cg):
    n_col, rows, width = qg.shape
    n_pb, crows, _ = cg.shape
    vmem = pl.BlockSpec(memory_space=pltpu.VMEM)
    block = (rows, width)
    dma = pltpu.SemaphoreType.DMA
    return pl.pallas_call(
        functools.partial(scatter_kernel, n_col, n_pb),
        out_shape=(jax.ShapeDtypeStruct(block, BF16), jax.ShapeDtypeStruct((crows, width), BF16)),
        in_specs=[vmem, vmem],
        out_specs=(vmem, vmem),
        scratch_shapes=[
            pltpu.VMEM((n_col, *block), BF16),
            pltpu.VMEM((n_col, *block), BF16),
            pltpu.VMEM((n_col, *block), BF16),
            pltpu.VMEM((n_col, *block), BF16),
            pltpu.VMEM((max(n_pb - 1, 1), crows, width), BF16),
        ]
        + [dma((n_col,))] * 6
        + [dma((n_pb,))] * 2,
        compiler_params=pltpu.CompilerParams(
            collective_id=2, has_side_effects=True, vmem_limit_bytes=60 * 2**20
        ),
        name="scatter",
    )(qg, cg)


def local(queries, candidates, grades, query_weights):
    n_col, n_pb = lax.axis_size("col"), lax.axis_size("pb")
    width = queries.shape[1]
    rows = queries.shape[0]
    scaling = 1.0 / math.sqrt(width)
    q_all, c_all = gather(queries, candidates, n_col, n_pb)
    c_block = c_all.reshape(-1, width)
    expo, stats = score(q_all, c_block, grades, scaling)
    merged = merge(stats, grades.shape[1] * n_col)
    losses = merged[:, 2 * GRADES].reshape(-1)
    weights = query_weights.reshape(n_col, 1, rows)
    qg, cg = slope(expo, grades, q_all, c_block, stats, merged, weights, scaling)
    query_grad, cand_grad = scatter(qg, cg.reshape(n_pb, -1, width))
    return (losses, query_grad, cand_grad)


def solution(mesh):
    in_specs = (P(("pb", "col"), None), P(("col", "pb"), None), P("pb", "col"), P("pb"))
    out_specs = (P("pb"), P(("pb", "col"), None), P(("col", "pb"), None))
    return jax.shard_map(local, mesh=mesh, in_specs=in_specs, out_specs=out_specs, check_vma=False)
```

time: 428 us -> 170 us (0.40)
  waiting for transfers between devices: 231 us -> 0 us
  Pallas kernels: 0 us -> 157 us
  blocking collectives: 86.4 us -> 0 us
  other arithmetic: 44.8 us -> 0 us
  matrix products: 34.6 us -> 0 us
  between operations: 13.9 us -> 0.69 us
    pallas_call x0 -> x5, Pallas kernels: none -> 157 us  [the longest x1 43 us: scatter(): pl.pallas_call(functools.partial(scatter_kernel, n_col, n_pb), out_shape=...]
    reduce_scatter x2 -> x0, waiting for transfers between devices: 149 us -> none  [the longest x1 105 us: local(): lax.psum_scatter(jnp.dot(slopes, cand_block, preferred_element_type=jnp.f...]
    all_gather x4 -> x0, blocking collectives: 86.4 us -> none  [combined_all(): everything = jax.tree.map(lambda part: lax.all_gather(part, axis), x)]
    all_gather x2 -> x0, waiting for transfers between devices: 80.1 us -> none  [the longest x1 52.6 us: local(): query_block = lax.all_gather(queries, 'col', axis=0, tiled=True)]
    dot_general x3 -> x0, matrix products: 34.6 us -> none  [the longest x1 19.5 us: local(): jnp.dot(query_block, cand_block.T, preferred_element_type=jnp.float32)]
    reduce_sum x1 -> x0, other arithmetic: 16.7 us -> none  [masses_from(): jnp.sum(jnp.where(members[bucket], expo, 0.0), axis=1)]
    add x34 -> x0, other arithmetic: 14.9 us -> none  [the longest x15 14.2 us: combine(): former[1] * jnp.exp(former[0] - merged)]
    convert_element_type x3 -> x0, other arithmetic: 12.5 us -> none  [the longest x1 8.7 us: local(): (query_weights[:, None] * (spread_rows(scaled_factors) * expo - 1.0)).ast...]
  transfers between devices with their start and end apart: 4 -> 0, of which waited for: 4 -> 0; matrix products, arithmetic and copies ran while one was open for 5% -> 0% of each run, Pallas kernels for 0% -> 0%
where the time goes in v1:
time: 170 us; the launch traced here: 169 us
  Pallas kernels  157 us (92%)
  local copies, waits for them, and re-layouts  12.1 us (7%)
    pallas_call x1, Pallas kernels, scatter(): pl.pallas_call(functools.partial(scatter_kernel, n_col, n_pb), out_shape=...  43 us
    pallas_call x1, Pallas kernels, gather(): pl.pallas_call(functools.partial(gather_kernel, n_col, n_pb), out_shape=(...  42.2 us
    pallas_call x1, Pallas kernels, score(): pl.pallas_call(functools.partial(score_kernel, scaling), grid=(n,), out_s...  30.7 us
    pallas_call x1, Pallas kernels, merge(): pl.pallas_call(functools.partial(merge_kernel, n_col, columns), out_shape...  20.8 us
    pallas_call x1, Pallas kernels, slope(): pl.pallas_call(functools.partial(slope_kernel, scaling, per), grid=(n //...  20 us
    unnamed x18, local copies, waits for them, and re-layouts  11.5 us

profile of v1, /device:TPU:0, one launch (start us, length us, event | category | flops | bytes accessed | tf_op | source)
XLA Modules:
  0.0 169.5 jit_solution(872588992632440728)
XLA Ops:
  0.6 42.2 %gather.1 = (bf16[16,128,1024]{2,1,0:T(8,128)(2,1)}, bf16[2,512,1024]{2,1,0:T(8,128)(2,1)}) custom-call(bf16[128,1024]{1,0:T(8,128)(2,1)} %q_ref.1, bf16[512,1024]{1,0:T(8,128)(2,1)} %c_ref.1), custom_call_target="tpu_custom_call" | custom-call | tf_op jit(solution)/shard_map/gather/pallas_call | solution.py:127
  42.8 0.0 copy-start
  42.8 2.2 %copy-done = bf16[16,128,1024]{2,1,0:T(8,128)(2,1)S(1)} copy-done((bf16[16,128,1024]{2,1,0:T(8,128)(2,1)S(1)}, bf16[16,128,1024]{2,1,0:T(8,128)(2,1)}, u32[]{:S(2)}) %copy-start) | copy-done | bytes 4194328
  45.0 0.0 copy-start.1
  45.0 1.6 copy-done.1
  46.6 0.0 copy-start.2
  46.6 0.0 copy-start.7
  46.6 30.7 %score.1 = (f32[2048,1024]{1,0:T(8,128)}, f32[16,16,128]{2,1,0:T(8,128)S(1)}) custom-call(bf16[16,128,1024]{2,1,0:T(8,128)(2,1)S(1)} %copy-done, bf16[1024,1024]{1,0:T(8,128)(2,1)S(1)} %bitcast.4, s32[2048,1024]{1,0:T(8,128)} %g_ref.3), custom_call_target="tpu_custom_call" | custom-call | tf_op jit(solution)/shard_map/score/pallas_call | solution.py:180
  77.3 0.0 copy-start.5
  77.3 0.7 copy-done.5
  78.0 20.8 %merge.1.f_ref = f32[16,16,128]{2,1,0:T(8,128)} custom-call(f32[16,16,128]{2,1,0:T(8,128)} %copy-done.5), custom_call_target="tpu_custom_call" | custom-call | tf_op jit(solution)/shard_map/merge/pallas_call | solution.py:266
  98.8 0.0 copy-done.2
  98.8 0.0 copy-done.7
  98.8 0.0 copy-start.4
  98.8 0.9 copy-done.4
  99.7 0.0 copy-start.6
  99.7 0.9 copy-done.6
  100.6 20.0 %slope.1 = (bf16[16,128,1024]{2,1,0:T(8,128)(2,1)}, bf16[1024,1024]{1,0:T(8,128)(2,1)S(1)}) custom-call(f32[2048,1024]{1,0:T(8,128)} %get-tuple-element.14.e_ref, s32[2048,1024]{1,0:T(8,128)} %g_ref.3, bf16[16,128,1024]{2,1,0:T(8,128)(2,1)} %get-tuple-element.11.q_ref, bf16[1024,1024]{1,0:T(8,128)(2,1)S(1)} %bitcast.5, f32[16,16,128]{2,1,0:T(8,128)S(1)} %copy-done.6, ...), custom_call_target="tpu_custom_call" | custom-call | tf_op jit(solution)/shard_map/slope/pallas_call | solution.py:327
  120.6 0.0 copy-start.3
  120.6 1.3 copy-done.3
  121.9 0.6 slice.3
  122.5 43.0 %scatter.1 = (bf16[128,1024]{1,0:T(8,128)(2,1)}, bf16[512,1024]{1,0:T(8,128)(2,1)}) custom-call(bf16[16,128,1024]{2,1,0:T(8,128)(2,1)} %get-tuple-element.15.qg, bf16[2,512,1024]{2,1,0:T(8,128)(2,1)} %bitcast.6), custom_call_target="tpu_custom_call" | custom-call | tf_op jit(solution)/shard_map/scatter/pallas_call | solution.py:427
  165.5 1.7 copy.9
  167.2 2.3 %copy.10 = bf16[512,1024]{1,0:T(8,128)(2,1)} copy(bf16[512,1024]{1,0:T(8,128)(2,1)} %get-tuple-element.24) | data formatting | bytes 2097152
Async XLA Ops:
  42.8 2.2 %copy-start = (bf16[16,128,1024]{2,1,0:T(8,128)(2,1)S(1)}, bf16[16,128,1024]{2,1,0:T(8,128)(2,1)}, u32[]{:S(2)}) copy-start(bf16[16,128,1024]{2,1,0:T(8,128)(2,1)} %get-tuple-element.11.q_ref) | copy-start | bytes 12582916
  45.0 1.6 copy-start.1
  46.6 52.2 %copy-start.2 = (bf16[2,512,1024]{2,1,0:T(8,128)(2,1)S(1)}, bf16[2,512,1024]{2,1,0:T(8,128)(2,1)}, u32[]{:S(2)}) copy-start(bf16[2,512,1024]{2,1,0:T(8,128)(2,1)} %get-tuple-element.12) | copy-start | bytes 6291460
  46.6 52.2 %copy-start.7 = (f32[2048]{0:T(1024)S(1)}, f32[2048]{0:T(1024)}, u32[]{:S(2)}) copy-start(f32[2048]{0:T(1024)} %param.7) | copy-start | bytes 24580
  77.3 0.7 copy-start.5
  98.8 0.9 copy-start.4
  99.7 0.9 copy-start.6
  120.6 1.3 copy-start.3

commit v2 on v1

--- a/solution.py
+++ b/solution.py
@@ -61,11 +61,40 @@
     )
 
 
-def gather_kernel(n_col, n_pb, q_ref, c_ref, q_all, c_all, q_send, q_recv, c_send, c_recv, own_sem):
+def score_tile(scaling, q, c, grades):
+    rows = grades.shape[0]
+    scores = lax.dot_general(q, c, (((1,), (1,)), ((), ())), preferred_element_type=F32) * scaling
+    lane = lax.broadcasted_iota(jnp.int32, (rows, rows), 1)
+    table = jnp.zeros((rows, rows), F32)
+    picked = jnp.zeros(scores.shape, F32)
+    for b in range(GRADES):
+        member = grades == b
+        highest = jnp.max(jnp.where(member, scores, LOWEST), axis=1, keepdims=True)
+        picked = jnp.where(member, highest, picked)
+        table = jnp.where(lane == b, highest, table)
+    expo = jnp.exp(scores - picked)
+    for b in range(GRADES):
+        member = grades == b
+        mass = jnp.sum(jnp.where(member, expo, 0.0), axis=1, keepdims=True)
+        count = jnp.sum(jnp.where(member, 1.0, 0.0), axis=1, keepdims=True)
+        table = jnp.where(lane == GRADES + b, mass, table)
+        table = jnp.where(lane == 2 * GRADES + b, count, table)
+    total = jnp.sum(scores, axis=1, keepdims=True)
+    table = jnp.where(lane == 3 * GRADES, total, table)
+    return expo, table.T[:STATS]
+
+
+def front_kernel(
+    n_col, n_pb, scaling, q_ref, c_ref, g_hbm, q_all, c_all, e_hbm, s_all,
+    g_all, e_all, q_send, q_recv, c_send, c_recv, own_sem, e_sem,
+):
     at = Place(n_col, n_pb)
+    rows, half = q_ref.shape[0], c_ref.shape[0]
+    grades_in = pltpu.make_async_copy(g_hbm, g_all, own_sem.at[0])
+    grades_in.start()
     own = [
-        pltpu.make_async_copy(q_ref, q_all.at[at.me], own_sem.at[0]),
-        pltpu.make_async_copy(c_ref, c_all.at[at.p], own_sem.at[1]),
+        pltpu.make_async_copy(q_ref, q_all.at[at.me], own_sem.at[1]),
+        pltpu.make_async_copy(c_ref, c_all.at[at.p], own_sem.at[2]),
     ]
     for copy in own:
         copy.start()
@@ -86,123 +115,144 @@
     def arrived(block):
         remote(q_ref, q_all.at[block], q_send.at[0], q_recv.at[block], dev(at.p, at.me)).wait_recv()
 
-    def spread(do, dm):
+    def forward(do, dm):
         block = at.index(do, dm, 0)
+        src = q_ref
         if do or dm:
             arrived(block)
             src = q_all.at[block]
-        else:
-            src = q_ref
         if dm == 0:
             if do == 0:
-                for d in range(1, at.outs):
+                for d in order[1:]:
                     push(src, block, dev(at.p, at.index(d, 0, 0)))
             for d in range(1, at.mids):
                 push(src, block, dev(at.p, at.index(0, d, 0)))
         for d in range(1, at.cores):
             push(src, block, dev(at.p, at.index(0, 0, d)))
 
+    def task(block, part):
+        span = pl.ds(pl.multiple_of(block * rows, rows), rows)
+        columns = pl.ds(pl.multiple_of(part * half, half), half)
+        expo, stats = score_tile(scaling, q_all[block], c_all[part], g_all[span, columns])
+        e_all[block, part] = expo
+        s_all[block, part] = stats
+        pltpu.make_async_copy(
+            e_all.at[block, part], e_hbm.at[block, part], e_sem.at[block, part]
+        ).start()
+
     order = [0] + sorted(range(1, at.outs), key=lambda d: min(d, at.outs - d))
-    for do in order:
-        spread(do, 0)
-    for do in order:
-        for dm in range(1, at.mids):
-            spread(do, dm)
-    for d in range(1, at.cores):
-        for do in order:
-            for dm in range(at.mids):
-                arrived(at.index(do, dm, d))
-    for d in range(1, n_pb):
-        other = lax.rem(at.p + d, n_pb)
-        remote(c_ref, c_all.at[other], c_send.at[0], c_recv.at[other], dev(at.p, at.me)).wait_recv()
+    last = order[-1]
+
+    def group(pairs):
+        first = pairs[0]
+        step = [b - a for a, b in zip(first, pairs[-1])]
+
+        def body(j, carry):
+            which = j // at.cores
+            dc = lax.rem(j, at.cores)
+            block = at.index(first[0] + which * step[0], first[1] + which * step[1], dc)
+
+            @pl.when(dc > 0)
+            def _():
+                arrived(block)
+
+            task(block, at.p)
+            return carry
+
+        lax.fori_loop(0, len(pairs) * at.cores, body, 0)
+
+    for k in range(at.outs):
+        pairs = [(order[k], 0)]
+        if k > 0 and at.mids > 1:
+            pairs.append((order[k - 1], 1))
+        for pair in pairs:
+            forward(*pair)
+        if k == 0:
+            for copy in own:
+                copy.wait()
+            grades_in.wait()
+        group(pairs)
+
+    def later(first, count):
+        for d in range(1, n_pb):
+            part = lax.rem(at.p + d, n_pb)
+
+            def body(j, carry):
+                do = last + 1 + j // (at.mids * at.cores)
+                dm = lax.rem(j // at.cores, at.mids)
+                task(at.index(do, dm, lax.rem(j, at.cores)), part)
+                return carry
+
+            if first == 0:
+                remote(
+                    c_ref, c_all.at[part], c_send.at[0], c_recv.at[part], dev(at.p, at.me)
+                ).wait_recv()
+            lax.fori_loop(first, first + count, body, 0)
+
+    tail = at.cores if at.mids > 1 else 0
+    if tail:
+        forward(last, 1)
+    later(0, n_col - tail)
+    if tail:
+        group([(last, 1)])
+        later(n_col - tail, tail)
+
+    def drain(j, carry):
+        for part in range(n_pb):
+            pltpu.make_async_copy(e_all.at[j, part], e_hbm.at[j, part], e_sem.at[j, part]).wait()
+        return carry
+
+    lax.fori_loop(0, n_col, drain, 0)
     for copy in sends + c_copies:
         copy.wait_send()
-    for copy in own:
-        copy.wait()
-
-
-def gather(q, c, n_col, n_pb):
+
+
+def front(q, c, grades, n_col, n_pb, scaling):
     vmem = pl.BlockSpec(memory_space=pltpu.VMEM)
     hbm = pl.BlockSpec(memory_space=pl.ANY)
+    rows, half = q.shape[0], c.shape[0]
+    e_shape = (n_col, n_pb, rows, half)
+    dma = pltpu.SemaphoreType.DMA
     return pl.pallas_call(
-        functools.partial(gather_kernel, n_col, n_pb),
+        functools.partial(front_kernel, n_col, n_pb, scaling),
         out_shape=(
             jax.ShapeDtypeStruct((n_col, *q.shape), q.dtype),
             jax.ShapeDtypeStruct((n_pb, *c.shape), c.dtype),
+            jax.ShapeDtypeStruct(e_shape, F32),
+            jax.ShapeDtypeStruct((n_col, n_pb, STATS, rows), F32),
         ),
-        in_specs=[vmem, vmem],
-        out_specs=(hbm, hbm),
+        in_specs=[vmem, vmem, hbm],
+        out_specs=(vmem, vmem, hbm, vmem),
         scratch_shapes=[
-            pltpu.SemaphoreType.DMA((2 * n_col,)),
-            pltpu.SemaphoreType.DMA((n_col,)),
-            pltpu.SemaphoreType.DMA((n_pb,)),
-            pltpu.SemaphoreType.DMA((n_pb,)),
-            pltpu.SemaphoreType.DMA((2,)),
+            pltpu.VMEM(grades.shape, jnp.int32),
+            pltpu.VMEM(e_shape, F32),
+            dma((2 * n_col,)),
+            dma((n_col,)),
+            dma((n_pb,)),
+            dma((n_pb,)),
+            dma((3,)),
+            dma((n_col, n_pb)),
         ],
-        compiler_params=pltpu.CompilerParams(collective_id=0, has_side_effects=True),
-        name="gather",
-    )(q, c)
-
-
-def score_kernel(scaling, q_ref, c_ref, g_ref, e_ref, s_ref):
-    rows = g_ref.shape[0]
-    scores = (
-        lax.dot_general(
-            q_ref[0], c_ref[...], (((1,), (1,)), ((), ())), preferred_element_type=F32
-        )
-        * scaling
-    )
-    grades = g_ref[...]
-    lane = lax.broadcasted_iota(jnp.int32, (rows, rows), 1)
-    table = jnp.zeros((rows, rows), F32)
-    picked = jnp.zeros(scores.shape, F32)
-    for b in range(GRADES):
-        member = grades == b
-        highest = jnp.max(jnp.where(member, scores, LOWEST), axis=1, keepdims=True)
-        picked = jnp.where(member, highest, picked)
-        table = jnp.where(lane == b, highest, table)
-    expo = jnp.exp(scores - picked)
-    e_ref[...] = expo
-    for b in range(GRADES):
-        member = grades == b
-        mass = jnp.sum(jnp.where(member, expo, 0.0), axis=1, keepdims=True)
-        count = jnp.sum(jnp.where(member, 1.0, 0.0), axis=1, keepdims=True)
-        table = jnp.where(lane == GRADES + b, mass, table)
-        table = jnp.where(lane == 2 * GRADES + b, count, table)
-    total = jnp.sum(scores, axis=1, keepdims=True)
-    table = jnp.where(lane == 3 * GRADES, total, table)
-    s_ref[0] = table.T[:STATS]
-
-
-def score(q_all, c_block, grades, scaling):
-    n, rows, width = q_all.shape
-    cols = c_block.shape[0]
-    return pl.pallas_call(
-        functools.partial(score_kernel, scaling),
-        grid=(n,),
-        out_shape=(
-            jax.ShapeDtypeStruct(grades.shape, F32),
-            jax.ShapeDtypeStruct((n, STATS, rows), F32),
+        compiler_params=pltpu.CompilerParams(
+            collective_id=0, has_side_effects=True, vmem_limit_bytes=56 * 2**20
         ),
-        in_specs=[
-            pl.BlockSpec((1, rows, width), lambda i: (i, 0, 0)),
-            pl.BlockSpec((cols, width), lambda i: (0, 0)),
-            pl.BlockSpec((rows, cols), lambda i: (i, 0)),
-        ],
-        out_specs=(
-            pl.BlockSpec((rows, cols), lambda i: (i, 0)),
-            pl.BlockSpec((1, STATS, rows), lambda i: (i, 0, 0)),
-        ),
-        compiler_params=pltpu.CompilerParams(vmem_limit_bytes=40 * 2**20),
-        name="score",
-    )(q_all, c_block, grades)
-
-
-def merge_kernel(n_col, columns, s_ref, all_ref, got, mine, send, recv, send2, recv2):
+        name="front",
+    )(q, c, grades)
+
+
+def merge_kernel(n_col, columns, parts_ref, all_ref, s_ref, got, mine, send, recv, send2, recv2):
     me = lax.axis_index("col")
     p = lax.axis_index("pb")
     others = [lax.rem(me + d, n_col) for d in range(1, n_col)]
     greet([dev(p, o) for o in others])
+    G = GRADES
+    for k in range(n_col):
+        parts = [parts_ref[k, h] for h in range(parts_ref.shape[1])]
+        top = parts[0][:G]
+        for part in parts[1:]:
+            top = jnp.maximum(top, part[:G])
+        mass = sum(part[G : 2 * G] * jnp.exp(part[:G] - top) for part in parts)
+        s_ref[k] = jnp.concatenate([top, mass, sum(part[2 * G :] for part in parts)], axis=0)
     copies = []
     for d, o in enumerate(others):
         copy = remote(s_ref.at[o], got.at[me], send.at[d], recv.at[me], dev(p, o))
@@ -211,7 +261,6 @@
     got[me] = s_ref[me]
     for o in others:
         remote(s_ref.at[o], got.at[o], send.at[0], recv.at[o], dev(p, o)).wait_recv()
-    G = GRADES
     maxima = got[0][:G]
     for k in range(1, n_col):
         maxima = jnp.maximum(maxima, got[k][:G])
@@ -261,15 +310,17 @@
 
 
 def merge(stats, columns):
-    n_col, _, rows = stats.shape
+    n_col, _, _, rows = stats.shape
+    shape = (n_col, STATS, rows)
     vmem = pl.BlockSpec(memory_space=pltpu.VMEM)
     return pl.pallas_call(
         functools.partial(merge_kernel, n_col, columns),
-        out_shape=jax.ShapeDtypeStruct(stats.shape, F32),
+        out_shape=jax.ShapeDtypeStruct(shape, F32),
         in_specs=[vmem],
         out_specs=vmem,
         scratch_shapes=[
-            pltpu.VMEM(stats.shape, F32),
+            pltpu.VMEM(shape, F32),
+            pltpu.VMEM(shape, F32),
             pltpu.VMEM((STATS, rows), F32),
             pltpu.SemaphoreType.DMA((n_col,)),
             pltpu.SemaphoreType.DMA((n_col,)),
@@ -284,17 +335,24 @@
 def slope_kernel(scaling, per, e_ref, g_ref, q_ref, c_ref, s_ref, f_ref, w_ref, qg_ref, cg_ref, acc):
     step = pl.program_id(0)
     G = GRADES
-    rows = s_ref.shape[2]
+    rows = s_ref.shape[3]
     pieces = []
+    n_pb = s_ref.shape[1]
+    half = e_ref.shape[3]
     for k in range(per):
-        local, merged, weight = s_ref[k], f_ref[k], w_ref[k]
-        scaled = weight * (merged[G : 2 * G] * jnp.exp(local[:G] - merged[:G]))
-        table = jnp.concatenate([scaled, weight, jnp.zeros((rows - G - 1, rows), F32)], axis=0).T
-        grades = g_ref[k * rows : (k + 1) * rows]
-        picked = jnp.broadcast_to(table[:, 0:1], grades.shape)
-        for b in range(1, G):
-            picked = jnp.where(grades == b, table[:, b : b + 1], picked)
-        slopes = picked * e_ref[k * rows : (k + 1) * rows] - table[:, G : G + 1]
+        merged, weight = f_ref[k], w_ref[k]
+        factor = weight * merged[G : 2 * G]
+        scaled = [factor * jnp.exp(s_ref[k, h, :G] - merged[:G]) for h in range(n_pb)]
+        pad = jnp.zeros((rows - n_pb * G - 1, rows), F32)
+        table = jnp.concatenate(scaled + [weight, pad], axis=0).T
+        sections = []
+        for h in range(n_pb):
+            grades = g_ref[k * rows : (k + 1) * rows, h * half : (h + 1) * half]
+            picked = jnp.broadcast_to(table[:, h * G : h * G + 1], grades.shape)
+            for b in range(1, G):
+                picked = jnp.where(grades == b, table[:, h * G + b : h * G + b + 1], picked)
+            sections.append(picked * e_ref[k, h] - table[:, n_pb * G : n_pb * G + 1])
+        slopes = jnp.concatenate(sections, axis=1)
         pieces.append(slopes.astype(BF16))
     slopes = jnp.concatenate(pieces, axis=0)
     part = jnp.dot(slopes, c_ref[...], preferred_element_type=F32) * scaling
@@ -324,6 +382,7 @@
     cols = c_block.shape[0]
     per = 2 if n % 2 == 0 else 1
     block3 = lambda a, b: pl.BlockSpec((per, a, b), lambda i: (i, 0, 0))
+    block4 = lambda a, b, c: pl.BlockSpec((per, a, b, c), lambda i: (i, 0, 0, 0))
     return pl.pallas_call(
         functools.partial(slope_kernel, scaling, per),
         grid=(n // per,),
@@ -332,11 +391,11 @@
             jax.ShapeDtypeStruct((cols, width), BF16),
         ),
         in_specs=[
-            pl.BlockSpec((per * rows, cols), lambda i: (i, 0)),
+            block4(*expo.shape[1:]),
             pl.BlockSpec((per * rows, cols), lambda i: (i, 0)),
             block3(rows, width),
             pl.BlockSpec((cols, width), lambda i: (0, 0)),
-            block3(STATS, rows),
+            block4(*stats.shape[1:]),
             block3(STATS, rows),
             block3(1, rows),
         ],
@@ -450,9 +509,8 @@
     width = queries.shape[1]
     rows = queries.shape[0]
     scaling = 1.0 / math.sqrt(width)
-    q_all, c_all = gather(queries, candidates, n_col, n_pb)
+    q_all, c_all, expo, stats = front(queries, candidates, grades, n_col, n_pb, scaling)
     c_block = c_all.reshape(-1, width)
-    expo, stats = score(q_all, c_block, grades, scaling)
     merged = merge(stats, grades.shape[1] * n_col)
     losses = merged[:, 2 * GRADES].reshape(-1)
     weights = query_weights.reshape(n_col, 1, rows)

time: 170 us -> 149 us (0.88)
  Pallas kernels: 157 us -> 138 us
  local copies, waits for them, and re-layouts: 12.1 us -> 9.33 us
    pallas_call x2 -> x1, Pallas kernels: 72.9 us -> 59.5 us  [front(): pl.pallas_call(functools.partial(front_kernel, n_col, n_pb, scaling), out...]
    pallas_call x1, Pallas kernels: 20.8 us -> 15.8 us  [merge(): pl.pallas_call(functools.partial(merge_kernel, n_col, columns), out_shape...]
    unnamed x18 -> x12, local copies, waits for them, and re-layouts: 11.5 us -> 8.72 us
where the time goes in v2:
time: 149 us; the launch traced here: 148 us
  Pallas kernels  138 us (93%)
  local copies, waits for them, and re-layouts  9.33 us (6%)
    pallas_call x1, Pallas kernels, front(): pl.pallas_call(functools.partial(front_kernel, n_col, n_pb, scaling), out...  59.5 us
    pallas_call x1, Pallas kernels, scatter(): pl.pallas_call(functools.partial(scatter_kernel, n_col, n_pb), out_shape=...  42.1 us
    pallas_call x1, Pallas kernels, slope(): pl.pallas_call(functools.partial(slope_kernel, scaling, per), grid=(n //...  21.1 us
    pallas_call x1, Pallas kernels, merge(): pl.pallas_call(functools.partial(merge_kernel, n_col, columns), out_shape...  15.8 us
    unnamed x12, local copies, waits for them, and re-layouts  8.72 us

profile of v2, /device:TPU:0, one launch (start us, length us, event | category | flops | bytes accessed | tf_op | source)
XLA Modules:
  0.0 148.4 jit_solution(17677314683969831911)
XLA Ops:
  0.6 0.0 copy-start.4
  0.6 59.5 %front.1 = (bf16[16,128,1024]{2,1,0:T(8,128)(2,1)}, bf16[2,512,1024]{2,1,0:T(8,128)(2,1)}, f32[16,2,128,512]{3,2,1,0:T(8,128)}, f32[16,2,16,128]{3,2,1,0:T(8,128)}) custom-call(bf16[128,1024]{1,0:T(8,128)(2,1)} %q_ref.1, bf16[512,1024]{1,0:T(8,128)(2,1)} %c_ref.1, s32[2048,1024]{1,0:T(8,128)} %g_ref.1), custom_call_target="tpu_custom_call" | custom-call | tf_op jit(solution)/shard_map/front/pallas_call | solution.py:216
  60.1 15.8 %merge.1.f_ref = f32[16,16,128]{2,1,0:T(8,128)} custom-call(f32[16,2,16,128]{3,2,1,0:T(8,128)} %get-tuple-element.11.parts_ref.s_ref), custom_call_target="tpu_custom_call" | custom-call | tf_op jit(solution)/shard_map/merge/pallas_call | solution.py:316
  75.9 0.0 copy-done.4
  75.9 0.0 copy-start.1
  75.9 1.6 %copy-done.1 = bf16[2,512,1024]{2,1,0:T(8,128)(2,1)S(1)} copy-done((bf16[2,512,1024]{2,1,0:T(8,128)(2,1)S(1)}, bf16[2,512,1024]{2,1,0:T(8,128)(2,1)}, u32[]{:S(2)}) %copy-start.1) | copy-done | bytes 2097176
  77.5 0.0 copy-start.2
  77.5 0.9 copy-done.2
  78.4 0.0 copy-start.3
  78.4 0.9 copy-done.3
  79.3 21.1 %slope.1 = (bf16[16,128,1024]{2,1,0:T(8,128)(2,1)}, bf16[1024,1024]{1,0:T(8,128)(2,1)S(1)}) custom-call(f32[16,2,128,512]{3,2,1,0:T(8,128)} %get-tuple-element.12.e_ref, s32[2048,1024]{1,0:T(8,128)} %g_ref.1, bf16[16,128,1024]{2,1,0:T(8,128)(2,1)} %get-tuple-element.13.q_ref, bf16[1024,1024]{1,0:T(8,128)(2,1)S(1)} %bitcast.5, ...), custom_call_target="tpu_custom_call" | custom-call | tf_op jit(solution)/shard_map/slope/pallas_call | solution.py:386
  100.5 0.0 copy-start
  100.5 1.3 copy-done
  101.8 0.6 slice.3
  102.4 42.1 %scatter.1 = (bf16[128,1024]{1,0:T(8,128)(2,1)}, bf16[512,1024]{1,0:T(8,128)(2,1)}) custom-call(bf16[16,128,1024]{2,1,0:T(8,128)(2,1)} %get-tuple-element.15.qg, bf16[2,512,1024]{2,1,0:T(8,128)(2,1)} %bitcast.4), custom_call_target="tpu_custom_call" | custom-call | tf_op jit(solution)/shard_map/scatter/pallas_call | solution.py:486
  144.5 1.7 %copy.9 = bf16[128,1024]{1,0:T(8,128)(2,1)} copy(bf16[128,1024]{1,0:T(8,128)(2,1)} %get-tuple-element.23) | data formatting | bytes 524288
  146.2 2.3 %copy.10 = bf16[512,1024]{1,0:T(8,128)(2,1)} copy(bf16[512,1024]{1,0:T(8,128)(2,1)} %get-tuple-element.24) | data formatting | bytes 2097152
Async XLA Ops:
  0.6 75.2 %copy-start.4 = (f32[2048]{0:T(1024)S(1)}, f32[2048]{0:T(1024)}, u32[]{:S(2)}) copy-start(f32[2048]{0:T(1024)} %param.7) | copy-start | bytes 24580
  75.9 1.6 %copy-start.1 = (bf16[2,512,1024]{2,1,0:T(8,128)(2,1)S(1)}, bf16[2,512,1024]{2,1,0:T(8,128)(2,1)}, u32[]{:S(2)}) copy-start(bf16[2,512,1024]{2,1,0:T(8,128)(2,1)} %get-tuple-element.14) | copy-start | bytes 6291460
  77.5 0.9 copy-start.2
  78.4 0.9 copy-start.3
  100.5 1.3 copy-start

commit v3 on v2

--- a/solution.py
+++ b/solution.py
@@ -76,9 +76,18 @@
     for b in range(GRADES):
         member = grades == b
         mass = jnp.sum(jnp.where(member, expo, 0.0), axis=1, keepdims=True)
-        count = jnp.sum(jnp.where(member, 1.0, 0.0), axis=1, keepdims=True)
         table = jnp.where(lane == GRADES + b, mass, table)
-        table = jnp.where(lane == 2 * GRADES + b, count, table)
+    assert scores.shape[1] < 4096
+    rest = jnp.full((rows, 1), float(scores.shape[1]), F32)
+    for b in range(0, GRADES - 1, 2):
+        pair = jnp.where(grades == b, 1.0, jnp.where(grades == b + 1, 4096.0, 0.0))
+        pair = jnp.sum(pair, axis=1, keepdims=True)
+        high = jnp.floor(pair * (1.0 / 4096.0))
+        low = pair - high * 4096.0
+        table = jnp.where(lane == 2 * GRADES + b, low, table)
+        table = jnp.where(lane == 2 * GRADES + b + 1, high, table)
+        rest = rest - low - high
+    table = jnp.where(lane == 3 * GRADES - 1, rest, table)
     total = jnp.sum(scores, axis=1, keepdims=True)
     table = jnp.where(lane == 3 * GRADES, total, table)
     return expo, table.T[:STATS]

time: 149 us -> 149 us (level)
  no operation moved by 1% of the time
where the time goes in v3:
time: 149 us; the launch traced here: 148 us
  Pallas kernels  138 us (93%)
  local copies, waits for them, and re-layouts  9.33 us (6%)
    pallas_call x1, Pallas kernels, front(): pl.pallas_call(functools.partial(front_kernel, n_col, n_pb, scaling), out...  59.4 us
    pallas_call x1, Pallas kernels, scatter(): pl.pallas_call(functools.partial(scatter_kernel, n_col, n_pb), out_shape=...  42.1 us
    pallas_call x1, Pallas kernels, slope(): pl.pallas_call(functools.partial(slope_kernel, scaling, per), grid=(n //...  21.1 us
    pallas_call x1, Pallas kernels, merge(): pl.pallas_call(functools.partial(merge_kernel, n_col, columns), out_shape...  15.8 us
    unnamed x12, local copies, waits for them, and re-layouts  8.72 us

profile of v3, /device:TPU:0, one launch (start us, length us, event | category | flops | bytes accessed | tf_op | source)
XLA Modules:
  0.0 148.4 jit_solution(17794237491519640038)
XLA Ops:
  0.6 0.0 copy-start.4
  0.6 59.4 %front.1 = (bf16[16,128,1024]{2,1,0:T(8,128)(2,1)}, bf16[2,512,1024]{2,1,0:T(8,128)(2,1)}, f32[16,2,128,512]{3,2,1,0:T(8,128)}, f32[16,2,16,128]{3,2,1,0:T(8,128)}) custom-call(bf16[128,1024]{1,0:T(8,128)(2,1)} %q_ref.1, bf16[512,1024]{1,0:T(8,128)(2,1)} %c_ref.1, s32[2048,1024]{1,0:T(8,128)} %g_ref.1), custom_call_target="tpu_custom_call" | custom-call | tf_op jit(solution)/shard_map/front/pallas_call | solution.py:225
  60.1 15.8 %merge.1.f_ref = f32[16,16,128]{2,1,0:T(8,128)} custom-call(f32[16,2,16,128]{3,2,1,0:T(8,128)} %get-tuple-element.11.parts_ref.s_ref), custom_call_target="tpu_custom_call" | custom-call | tf_op jit(solution)/shard_map/merge/pallas_call | solution.py:325
  75.8 0.0 copy-done.4
  75.8 0.0 copy-start.1
  75.8 1.6 %copy-done.1 = bf16[2,512,1024]{2,1,0:T(8,128)(2,1)S(1)} copy-done((bf16[2,512,1024]{2,1,0:T(8,128)(2,1)S(1)}, bf16[2,512,1024]{2,1,0:T(8,128)(2,1)}, u32[]{:S(2)}) %copy-start.1) | copy-done | bytes 2097176
  77.4 0.0 copy-start.2
  77.4 0.9 copy-done.2
  78.4 0.0 copy-start.3
  78.4 0.9 copy-done.3
  79.3 21.1 %slope.1 = (bf16[16,128,1024]{2,1,0:T(8,128)(2,1)}, bf16[1024,1024]{1,0:T(8,128)(2,1)S(1)}) custom-call(f32[16,2,128,512]{3,2,1,0:T(8,128)} %get-tuple-element.12.e_ref, s32[2048,1024]{1,0:T(8,128)} %g_ref.1, bf16[16,128,1024]{2,1,0:T(8,128)(2,1)} %get-tuple-element.13.q_ref, bf16[1024,1024]{1,0:T(8,128)(2,1)S(1)} %bitcast.5, ...), custom_call_target="tpu_custom_call" | custom-call | tf_op jit(solution)/shard_map/slope/pallas_call | solution.py:395
  100.4 0.0 copy-start
  100.4 1.3 copy-done
  101.8 0.6 slice.3
  102.4 42.1 %scatter.1 = (bf16[128,1024]{1,0:T(8,128)(2,1)}, bf16[512,1024]{1,0:T(8,128)(2,1)}) custom-call(bf16[16,128,1024]{2,1,0:T(8,128)(2,1)} %get-tuple-element.15.qg, bf16[2,512,1024]{2,1,0:T(8,128)(2,1)} %bitcast.4), custom_call_target="tpu_custom_call" | custom-call | tf_op jit(solution)/shard_map/scatter/pallas_call | solution.py:495
  144.5 1.7 %copy.9 = bf16[128,1024]{1,0:T(8,128)(2,1)} copy(bf16[128,1024]{1,0:T(8,128)(2,1)} %get-tuple-element.23) | data formatting | bytes 524288
  146.1 2.3 %copy.10 = bf16[512,1024]{1,0:T(8,128)(2,1)} copy(bf16[512,1024]{1,0:T(8,128)(2,1)} %get-tuple-element.24) | data formatting | bytes 2097152
Async XLA Ops:
  0.6 75.2 %copy-start.4 = (f32[2048]{0:T(1024)S(1)}, f32[2048]{0:T(1024)}, u32[]{:S(2)}) copy-start(f32[2048]{0:T(1024)} %param.7) | copy-start | bytes 24580
  75.8 1.6 %copy-start.1 = (bf16[2,512,1024]{2,1,0:T(8,128)(2,1)S(1)}, bf16[2,512,1024]{2,1,0:T(8,128)(2,1)}, u32[]{:S(2)}) copy-start(bf16[2,512,1024]{2,1,0:T(8,128)(2,1)} %get-tuple-element.14) | copy-start | bytes 6291460
  77.4 0.9 copy-start.2
  78.4 0.9 copy-start.3
  100.4 1.3 copy-start
